TPU v7x, 256 devices: a whole 4x4x8 slice. The times are simulated.
256 devices in a mesh: grp: 4 (over z_lo), tp: 32 (over x, y, z_hi), rep: 2 (over core).
Axes of the slice: x: 4, y: 4, z: 8 (z_hi: 2, z_lo: 4; z = z_hi * 4 + z_lo), core: 2. Of those that a mesh axis runs over, the one named last changes fastest.
Arguments:
- query_rows: bfloat16 [32, 1024, 2048], P('tp', ('grp', 'rep')), may hold values from -120 to 120
- key_rows: bfloat16 [32, 1024, 512], P('tp', ('grp', 'rep')), may hold values from -6 to 6, as said below
- value_rows: bfloat16 [32, 1024, 512], P('tp', ('grp', 'rep')), may hold values from -6 to 6
- teacher_codes: bfloat16 [32, 1024, 4096], P(None, ('grp', 'rep'), 'tp'), may hold values from -6 to 6
- teacher_scales: bfloat16 [32, 1024, 32], P(None, ('grp', 'rep'), 'tp'), may hold values from 0.099609375 to 1
- projection: bfloat16 [2048, 4096], P(None, ('grp', 'rep')), may hold values from -0.125 to 0.125
Outputs:
- grad_query: bfloat16 [32, 1024, 2048], P('tp', ('grp', 'rep'))
- grad_key: bfloat16 [32, 1024, 512], P('tp', ('grp', 'rep'))
- grad_value: bfloat16 [32, 1024, 512], P('tp', ('grp', 'rep'))
Inputs may be any that keep to these rules, and one draw needn't show every extreme that they name: `key_rows`: keys of every head.
All inputs are finite; a program needn't handle non-finite values.
Results may differ from a plain program's by a relative error of at most 0.014.
Values may be sent and summed in bfloat16 or wider, within the bound.
No kernel may reach another device: no remote copies, remote signals or barrier semaphores. Data moves between devices by JAX's collectives and lax.ppermute only.
A program may use at most 128 MiB of HBM per device.

v0:
```python
import math
import jax
import jax.numpy as jnp
from jax import lax
from jax.sharding import PartitionSpec as P

HEADS = 16
KV_HEADS = 4
HEAD_DIM = 128
QBLOCK = 128
masked_low = -1e30


def in_one_piece(arrays, axis, dim, along):
    widths = [a.shape[along] for a in arrays]
    both = jnp.concatenate(arrays, axis=along)
    whole = lax.all_gather(both, axis, axis=dim, tiled=True)
    return tuple(jnp.split(whole, [sum(widths[:k]) for k in range(1, len(widths))], axis=along))


def in_one_piece_2(arrays, axis, dim, along):
    widths = [a.shape[along] for a in arrays]
    both = jnp.concatenate(arrays, axis=along)
    whole = lax.psum_scatter(both, axis, scatter_dimension=dim, tiled=True)
    return tuple(jnp.split(whole, [sum(widths[:k]) for k in range(1, len(widths))], axis=along))


def shards(query_rows, key_rows, value_rows, teacher_codes, teacher_scales, projection):
    rows_dev = query_rows.shape[1]
    group_size = HEADS // KV_HEADS
    inv_root = 1.0 / math.sqrt(HEAD_DIM)
    keys_all, values_all = in_one_piece((key_rows, value_rows), ("grp", "rep"), 1, 0)
    length = keys_all.shape[1]
    key_block = min(1024, length)
    my_index = lax.axis_index(("grp", "rep"))
    first_row = my_index * rows_dev
    needed = (first_row + rows_dev + key_block - 1) // key_block
    queries = query_rows[0].reshape(rows_dev, KV_HEADS, group_size, HEAD_DIM).transpose(1, 2, 0, 3)
    key_heads = keys_all[0].reshape(length, KV_HEADS, HEAD_DIM).transpose(1, 0, 2)
    value_heads = values_all[0].reshape(length, KV_HEADS, HEAD_DIM).transpose(1, 0, 2)
    row_pos = first_row + jnp.arange(rows_dev, dtype=jnp.int32)
    slab_codes, slab_scales = (
        lax.all_to_all(teacher_codes, "tp", split_axis=0, concat_axis=2, tiled=True),
        lax.all_to_all(teacher_scales, "tp", split_axis=0, concat_axis=2, tiled=True),
    )

    def block_scores(block_index):
        offset = block_index * key_block
        raw_scores = (
            jnp.einsum("hgqd,hkd->hgqk", queries, key_heads, preferred_element_type=jnp.float32)
            * inv_root
        )
        col_pos = offset + jnp.arange(key_block, dtype=jnp.int32)
        allowed = col_pos[None, :] <= row_pos[:, None]
        return (jnp.where(allowed, raw_scores, masked_low), key_heads, value_heads)

    def stats_step(block_index, running):
        row_peak, row_total = running
        scores, key_part, value_part = block_scores(block_index)
        new_peak = jnp.maximum(row_peak, scores.max(-1))
        row_total = row_total * jnp.exp(row_peak - new_peak) + jnp.exp(
            scores - new_peak[..., None]
        ).sum(-1)
        return (new_peak, row_total)

    stat_shape = (KV_HEADS, group_size, rows_dev)
    row_peak, row_total = lax.fori_loop(
        0,
        needed,
        stats_step,
        (jnp.full(stat_shape, masked_low, jnp.float32), jnp.zeros(stat_shape, jnp.float32)),
    )

    def block_probs(scores):
        return jnp.exp(scores - row_peak[..., None]) / row_total[..., None]

    def output_step(block_index, running):
        scores, key_part, value_part = block_scores(block_index)
        prob_low = block_probs(scores).astype(jnp.bfloat16)
        return running + jnp.einsum(
            "hgqk,hkd->hgqd", prob_low, value_part, preferred_element_type=jnp.float32
        )

    attn_wide = lax.fori_loop(
        0, needed, output_step, jnp.zeros((KV_HEADS, group_size, rows_dev, HEAD_DIM), jnp.float32)
    )
    attn_low = (
        attn_wide.transpose(2, 0, 1, 3).reshape(rows_dev, HEADS * HEAD_DIM).astype(jnp.bfloat16)
    )
    col_width = projection.shape[1]
    shard_piece = lax.all_gather(projection, ("grp", "rep"), axis=1, tiled=True)
    pieces = shard_piece.shape[1] // col_width
    shaped = shard_piece.reshape(shard_piece.shape[0], pieces, col_width)
    approx = jnp.einsum("td,dsc->tsc", attn_low, shaped, preferred_element_type=jnp.float32)
    code_rows = slab_codes[0].astype(jnp.float32)
    scale_rows = slab_scales[0].astype(jnp.float32)
    target = (code_rows.reshape(rows_dev, -1, QBLOCK) * scale_rows[..., None]).reshape(
        rows_dev, pieces, col_width
    )
    errors = (approx - target).astype(jnp.bfloat16)
    partial_terms = jnp.einsum(
        "tsc,dsc->std", errors, shaped, preferred_element_type=jnp.float32
    ).astype(jnp.bfloat16)
    grad_attn = partial_terms.astype(jnp.float32).sum(0)
    grad_low = grad_attn.astype(jnp.bfloat16)
    grad_heads = grad_low.reshape(rows_dev, KV_HEADS, group_size, HEAD_DIM).transpose(1, 2, 0, 3)
    row_delta = (grad_heads.astype(jnp.float32) * attn_wide).sum(-1)

    def back_step(block_index, running):
        grad_queries, grad_keys, grad_values = running
        scores, key_part, value_part = block_scores(block_index)
        probs = block_probs(scores)
        prob_low = probs.astype(jnp.bfloat16)
        grad_prob = jnp.einsum(
            "hgqd,hkd->hgqk", grad_heads, value_part, preferred_element_type=jnp.float32
        )
        grad_score = (probs * (grad_prob - row_delta[..., None]) * inv_root).astype(jnp.bfloat16)
        grad_queries = grad_queries + jnp.einsum(
            "hgqk,hkd->hgqd", grad_score, key_part, preferred_element_type=jnp.float32
        )
        key_piece = jnp.einsum(
            "hgqk,hgqd->hkd", grad_score, queries, preferred_element_type=jnp.float32
        )
        value_piece = jnp.einsum(
            "hgqk,hgqd->hkd", prob_low, grad_heads, preferred_element_type=jnp.float32
        )
        grad_keys = key_piece
        grad_values = value_piece
        return (grad_queries, grad_keys, grad_values)

    zeros_kv = jnp.zeros((KV_HEADS, length, HEAD_DIM), jnp.float32)
    grad_queries, grad_keys, grad_values = lax.fori_loop(
        0,
        needed,
        back_step,
        (jnp.zeros((KV_HEADS, group_size, rows_dev, HEAD_DIM), jnp.float32), zeros_kv, zeros_kv),
    )
    key_terms = grad_keys.transpose(1, 0, 2).reshape(1, length, KV_HEADS * HEAD_DIM)
    value_terms = grad_values.transpose(1, 0, 2).reshape(1, length, KV_HEADS * HEAD_DIM)
    key_grad, value_grad = tuple(
        (
            part.astype(jnp.float32)
            for part in in_one_piece_2(
                (key_terms.astype(jnp.bfloat16), value_terms.astype(jnp.bfloat16)),
                ("grp", "rep"),
                1,
                0,
            )
        )
    )
    query_grad = (
        grad_queries.transpose(2, 0, 1, 3)
        .reshape(1, rows_dev, HEADS * HEAD_DIM)
        .astype(jnp.bfloat16)
    )
    return (query_grad, key_grad.astype(jnp.bfloat16), value_grad.astype(jnp.bfloat16))


def solution(mesh):
    placed = (
        P("tp", ("grp", "rep"), None),
        P("tp", ("grp", "rep"), None),
        P("tp", ("grp", "rep"), None),
        P(None, ("grp", "rep"), "tp"),
        P(None, ("grp", "rep"), "tp"),
        P(None, ("grp", "rep")),
    )
    return jax.shard_map(
        shards,
        mesh=mesh,
        in_specs=placed,
        out_specs=(
            P("tp", ("grp", "rep"), None),
            P("tp", ("grp", "rep"), None),
            P("tp", ("grp", "rep"), None),
        ),
        check_vma=False,
    )
```

profile of v0, /device:TPU:4, one launch (start us, length us, event | category | flops | bytes accessed | tf_op | source)
XLA Modules:
  0.0 334.3 jit_solution(7673649836879439004)
XLA Ops:
  10.1 4.0 %copy.49 = bf16[2048,512]{0,1:T(8,128)(2,1)} copy(bf16[2048,512]{1,0:T(8,128)(2,1)} %param.17) | data formatting | bytes 4194304 | tf_op args[5]
  14.1 1.3 copy.53
  15.4 14.2 %all-to-all-start.1 = ((bf16[32,128,1]{1,2,0:T(2,128)(2,1)}), bf16[32,128,1]{1,2,0:T(2,128)(2,1)S(1)}, u32[]{:S(2)}, u32[]{:S(2)}) async-start(bf16[32,128,1]{1,2,0:T(2,128)(2,1)} %copy.53), calls=%async_computation.1 | async-start | bytes 32768 | tf_op jit(solution)/shard_map/all_to_all | solution.py:44
  29.7 2.3 copy.52
  31.9 7.8 %all-to-all-done.1 = bf16[32,128,1]{1,2,0:T(2,128)(2,1)S(1)} async-done(((bf16[32,128,1]{1,2,0:T(2,128)(2,1)}), bf16[32,128,1]{1,2,0:T(2,128)(2,1)S(1)}, u32[]{:S(2)}, u32[]{:S(2)}) %all-to-all-start.1) | async-done | bytes 8224 | tf_op jit(solution)/shard_map/all_to_all | solution.py:44
  39.7 6.7 %all-to-all-start = ((bf16[32,128,128]{1,2,0:T(8,128)(2,1)}), bf16[32,128,128]{1,2,0:T(8,128)(2,1)}, u32[]{:S(2)}, u32[]{:S(2)}) async-start(bf16[32,128,128]{1,2,0:T(8,128)(2,1)} %copy.52), calls=%async_computation | async-start | bytes 2097152 | tf_op jit(solution)/shard_map/all_to_all | solution.py:43
  47.2 1.8 copy.55
  49.0 22.4 %all-to-all-done = bf16[32,128,128]{1,2,0:T(8,128)(2,1)} async-done(((bf16[32,128,128]{1,2,0:T(8,128)(2,1)}), bf16[32,128,128]{1,2,0:T(8,128)(2,1)}, u32[]{:S(2)}, u32[]{:S(2)}) %all-to-all-start) | async-done | bytes 1048608 | tf_op jit(solution)/shard_map/all_to_all | solution.py:43
  71.5 1.5 bitcast_convert_fusion
  72.9 1.8 copy.54
  74.8 3.2 fusion.26
  78.6 1.6 copy.47
  80.2 4.2 %while.39 = (s32[]{:T(128)}, f32[4,4,128]{2,1,0:T(4,128)S(1)}, f32[4,4,128]{2,1,0:T(4,128)S(1)}, s32[]{:T(128)}, bf16[4,4,128,128]{3,2,1,0:T(8,128)(2,1)S(1)}, /...) while((s32[]{:T(128)}, f32[4,4,128]{2,1,0:T(4,128)S(1)}, ...), condition=%wide.region_3.4_spmd.clone, body=%wide.region_0.3_spmd.clone.sunk | while | flops 551687296 | bytes 18859120 | solution.py:67
  80.4 1.6 fusion.66
  82.0 2.3 exponential_reduce_fusion.2
  85.6 5.8 %while.40 = (s32[]{:T(128)}, f32[4,4,128,128]{3,2,1,0:T(8,128)}, s32[]{:T(128)}, bf16[4,4,128,128]{3,2,1,0:T(8,128)(2,1)S(1)}, bf16[4,1024,128]{2,1,0:T(8,128)(2...) while((s32[]{:T(128)}, f32[4,4,128,128]{3,2,1,0:T(8,128)}, ...), condition=%wide.region_5.6_spmd.clone, body=%wide.region_4.5_spmd.clone.sunk | while | flops 1084621952 | bytes 5006465 | solution.py:84
  85.7 5.7 %fusion.70 = f32[4,4,128,128]{3,2,1,0:T(8,128)} fusion(f32[4,4,128,128]{3,2,1,0:T(8,128)} %get-tuple-element.573, f32[4,4,128]{2,1,0:T(4,128)S(1)} %get-tuple-element.589, f32[4,4,128]{2,1,0:T(4,128)S(1)} %get-tuple-element.588, pred[128,1024]{1,0:T(8,128)(4,1)S(1)} %broadcast_compare_fusion.7, bf16[4,4,128,128]{3,2,1,0:T(8,128)(2,1)S(1)} %get-tuple-element.586, ...), kind=kOutput, calls=%fused_computation.15.clone.1 | convolution fusion | flops 1084489728 | bytes 4866048 | tf_op jit(solution)/shard_map/while/body/hgqk,hkd->hgqd/dot_general | solution.py:80
  91.4 3.0 copy.48
  95.7 141.3 %all-gather.5.cloned.1.call-done = bf16[2048,4096]{0,1:T(8,128)(2,1)} async-done(((bf16[2048,512]{0,1:T(8,128)(2,1)}), bf16[2048,4096]{0,1:T(8,128)(2,1)}) %all-gather.5.cloned.1.call-update) | async-done | bytes 16777232 | tf_op jit(solution)/shard_map/all_gather | solution.py:91
  237.0 21.9 %convert_reduce_fusion = bf16[128,2048]{1,0:T(8,128)(2,1)} fusion(bf16[2048,8,512]{0,2,1:T(8,128)(2,1)} %bitcast.142, f32[128,8,512]{2,0,1:T(8,128)} %copy.54, f32[128,8,512]{2,0,1:T(8,128)} %copy.55, bf16[128,2048,1]{0,1,2:T(8,128)(2,1)S(1)} %bitcast.145), kind=kOutput, calls=%fused_computation.36 | convolution fusion | flops 4300472320 | bytes 22020096 | tf_op jit(solution)/shard_map/tsc,dsc->std/dot_general | solution.py:101
  260.2 1.5 multiply_reduce_fusion
  265.4 11.0 %while.41 = (s32[]{:T(128)}, f32[4,4,128,128]{3,2,1,0:T(8,128)S(1)}, bf16[4,1024,128]{2,1,0:T(8,128)(2,1)}, bf16[4,1024,128]{2,1,0:T(8,128)(2,1)}, s32[]{:T(128)...) while((s32[]{:T(128)}, ...), condition=%wide.region_9.10_spmd.clone, body=%wide.region_8.9_spmd.clone.sunk | while | flops 2703623168 | bytes 51676348 | solution.py:132
  265.6 2.8 exponential_divide_fusion.2
  268.4 1.5 multiply_convert_fusion.2
  269.9 1.3 convolution_add_fusion.2
  271.2 2.6 convolution_bitcast_fusion.2
  273.8 2.6 fusion.81
  276.4 2.0 copy.64
  279.7 2.0 copy.65
  282.9 3.1 pad_maximum_fusion
  287.7 38.4 %reduce-scatter.2.cloned.1.call-done = bf16[2,128,512]{2,1,0:T(8,128)(2,1)} async-done(((bf16[2,1024,512]{2,1,0:T(8,128)(2,1)}), bf16[2,128,512]{2,1,0:T(8,128)(2,1)}) %reduce-scatter.2.cloned.1.call-update) | async-done | bytes 262160 | tf_op jit(solution)/shard_map/reduce_scatter | solution.py:24
  326.1 1.7 fusion.27
  (49 shorter events, 16.4 us)
Async XLA Ops:
  7.2 39.3 %copy-start.3 = (bf16[1,128,2048]{2,1,0:T(8,128)(2,1)S(1)}, bf16[1,128,2048]{2,1,0:T(8,128)(2,1)}, u32[]{:S(2)}) copy-start(bf16[1,128,2048]{2,1,0:T(8,128)(2,1)} %param.12) | copy-start | bytes 1572868
  7.2 67.6 %all-gather.3.cloned.1.call-start = ((), (), s32[]{:S(2)}) async-start(), calls=%async_computation.3 | async-start | bytes 2359296 | tf_op jit(solution)/shard_map/all_gather | solution.py:17
  10.1 226.9 %all-gather.5.cloned.1.call-start = ((), (), s32[]{:S(2)}) async-start(), calls=%async_computation.4 | async-start | bytes 18874368 | tf_op jit(solution)/shard_map/all_gather | solution.py:91
  15.4 24.3 %all-to-all-start.1 = ((bf16[32,128,1]{1,2,0:T(2,128)(2,1)}), bf16[32,128,1]{1,2,0:T(2,128)(2,1)S(1)}, u32[]{:S(2)}, u32[]{:S(2)}) async-start(bf16[32,128,1]{1,2,0:T(2,128)(2,1)} %copy.53), calls=%async_computation.1 | async-start | bytes 32768 | tf_op jit(solution)/shard_map/all_to_all | solution.py:44
  39.7 31.7 %all-to-all-start = ((bf16[32,128,128]{1,2,0:T(8,128)(2,1)}), bf16[32,128,128]{1,2,0:T(8,128)(2,1)}, u32[]{:S(2)}, u32[]{:S(2)}) async-start(bf16[32,128,128]{1,2,0:T(8,128)(2,1)} %copy.52), calls=%async_computation | async-start | bytes 2097152 | tf_op jit(solution)/shard_map/all_to_all | solution.py:43
  46.4 279.7 %reduce-scatter.2.cloned.1.call-start = ((), (), s32[]{:S(2)}) async-start(), calls=%async_computation.5 | async-start | bytes 2359296 | tf_op jit(solution)/shard_map/reduce_scatter | solution.py:24
  91.4 167.5 %copy-start = (bf16[4,1024,128]{2,1,0:T(8,128)(2,1)}, bf16[4,1024,128]{2,1,0:T(8,128)(2,1)S(1)}, u32[]{:S(2)}) copy-start(bf16[4,1024,128]{2,1,0:T(8,128)(2,1)S(1)} %get-tuple-element.647) | copy-start | bytes 3145732
  260.2 1.6 copy-start.2
  265.6 2.8 copy-start.1
Sparse Core Ops, SparseCore 0:
  10.3 46.4 all-gather.2
  58.5 178.4 all-gather.4
  286.2 39.9 reduce-scatter.1
where the time goes:
time: 335 us; the launch traced here: 334 us
  waiting for transfers between devices  210 us (63%)
  matrix products  39.9 us (12%)
  local copies, waits for them, and re-layouts  38.4 us (11%)
  starting transfers between devices  21 us (6%)
  between operations  13.9 us (4%)
  other arithmetic  11 us (3%)
    all_gather x1, waiting for transfers between devices, shards(): shard_piece = lax.all_gather(projection, ('grp', 'rep'), axis=1, tiled=True)  141 us
    reduce_scatter x1, waiting for transfers between devices, in_one_piece_2(): whole = lax.psum_scatter(both, axis, scatter_dimension=dim, tiled=True)  38.4 us
    all_to_all x1, waiting for transfers between devices, shards(): lax.all_to_all(teacher_codes, 'tp', split_axis=0, concat_axis=2, tiled=True)  22.4 us
    dot_general x1, matrix products, shards(): jnp.einsum('tsc,dsc->std', errors, shaped, preferred_element_type=jnp.flo...  21.9 us
    all_to_all x1, starting transfers between devices, shards(): lax.all_to_all(teacher_scales, 'tp', split_axis=0, concat_axis=2, tiled=T...  14.2 us
    unnamed x16, local copies, waits for them, and re-layouts  13.8 us
    all_to_all x1, waiting for transfers between devices, shards(): lax.all_to_all(teacher_scales, 'tp', split_axis=0, concat_axis=2, tiled=T...  7.78 us
  transfers between devices with their start and end apart: 5, of which 4 were waited for; matrix products, arithmetic and copies ran while one was open for 11% of the time, Pallas kernels for 0%

commit v1 on v0

--- a/solution.py
+++ b/solution.py
@@ -88,7 +88,12 @@
         attn_wide.transpose(2, 0, 1, 3).reshape(rows_dev, HEADS * HEAD_DIM).astype(jnp.bfloat16)
     )
     col_width = projection.shape[1]
-    shard_piece = lax.all_gather(projection, ("grp", "rep"), axis=1, tiled=True)
+    shard_piece = jnp.concatenate(
+        lax.all_to_all(
+            jnp.stack([projection] * lax.axis_size(("grp", "rep"))), ("grp", "rep"), 0, 0
+        ),
+        axis=1,
+    )
     pieces = shard_piece.shape[1] // col_width
     shaped = shard_piece.reshape(shard_piece.shape[0], pieces, col_width)
     approx = jnp.einsum("td,dsc->tsc", attn_low, shaped, preferred_element_type=jnp.float32)

time: 335 us -> 558 us (1.67)
  waiting for transfers between devices: 210 us -> 400 us
  blocking collectives: 0 us -> 26.2 us
    all_to_all x1, waiting for transfers between devices: 22.4 us -> 256 us  [shards(): lax.all_to_all(jnp.stack([projection] * lax.axis_size(('grp', 'rep'))), (...]
    all_gather x1 -> x0, waiting for transfers between devices: 141 us -> none  [shards(): shard_piece = lax.all_gather(projection, ('grp', 'rep'), axis=1, tiled=True)]
    all_gather x1, waiting for transfers between devices: 0.01 us -> 99.8 us  [in_one_piece(): whole = lax.all_gather(both, axis, axis=dim, tiled=True)]
    all_to_all x0 -> x1, blocking collectives: none -> 26.2 us  [shards(): lax.all_to_all(teacher_codes, 'tp', split_axis=0, concat_axis=2, tiled=True)]
    another operation x2 -> x3, local copies, waits for them, and re-layouts: 1.27 us -> 8.02 us  [the longest x1 6.82 us: shards(): jnp.stack([projection] * lax.axis_size(('grp', 'rep')))]
    unnamed x16 -> x19, local copies, waits for them, and re-layouts: 13.8 us -> 7.33 us
  transfers between devices with their start and end apart: 5 -> 4, of which waited for: 4 -> 4; matrix products, arithmetic and copies ran while one was open for 11% -> 5% of each run, Pallas kernels for 0% -> 0%
where the time goes in v1:
time: 558 us
  waiting for transfers between devices  400 us (72%)
  matrix products  42 us (8%)
  local copies, waits for them, and re-layouts  38.2 us (7%)
  blocking collectives  26.2 us (5%)
  starting transfers between devices  26 us (5%)
  between operations  14.3 us (3%)
  other arithmetic  11 us (2%)
    all_to_all x1, waiting for transfers between devices, shards(): lax.all_to_all(jnp.stack([projection] * lax.axis_size(('grp', 'rep'))), (...  256 us
    all_gather x1, waiting for transfers between devices, in_one_piece(): whole = lax.all_gather(both, axis, axis=dim, tiled=True)  99.8 us
    reduce_scatter x1, waiting for transfers between devices, in_one_piece_2(): whole = lax.psum_scatter(both, axis, scatter_dimension=dim, tiled=True)  35.1 us
    all_to_all x1, blocking collectives, shards(): lax.all_to_all(teacher_codes, 'tp', split_axis=0, concat_axis=2, tiled=True)  26.2 us
    dot_general x1, matrix products, shards(): jnp.einsum('tsc,dsc->std', errors, shaped, preferred_element_type=jnp.flo...  24.1 us
    all_to_all x1, starting transfers between devices, shards(): lax.all_to_all(teacher_scales, 'tp', split_axis=0, concat_axis=2, tiled=T...  14.2 us
    all_to_all x1, starting transfers between devices, shards(): lax.all_to_all(jnp.stack([projection] * lax.axis_size(('grp', 'rep'))), (...  11.7 us
  transfers between devices with their start and end apart: 4, of which 4 were waited for; matrix products, arithmetic and copies ran while one was open for 5% of the time, Pallas kernels for 0%

profile of v1, /device:TPU:4, one launch (start us, length us, event | category | flops | bytes accessed | tf_op | source)
XLA Modules:
  0.0 557.6 jit_solution(12981331852601185672)
XLA Ops:
  8.5 14.2 %all-to-all-start.2 = ((bf16[32,128,1]{1,2,0:T(2,128)(2,1)}), bf16[32,128,1]{1,2,0:T(2,128)(2,1)S(1)}, u32[]{:S(2)}, u32[]{:S(2)}) async-start(bf16[32,128,1]{1,2,0:T(2,128)(2,1)} %copy.49), calls=%async_computation.2 | async-start | bytes 32768 | tf_op jit(solution)/shard_map/all_to_all | solution.py:44
  22.7 1.6 copy.48
  24.3 8.4 %all-to-all-done.2 = bf16[32,128,1]{1,2,0:T(2,128)(2,1)S(1)} async-done(((bf16[32,128,1]{1,2,0:T(2,128)(2,1)}), bf16[32,128,1]{1,2,0:T(2,128)(2,1)S(1)}, u32[]{:S(2)}, u32[]{:S(2)}) %all-to-all-start.2) | async-done | bytes 8224 | tf_op jit(solution)/shard_map/all_to_all | solution.py:44
  32.7 26.2 %all_to_all.23 = bf16[32,128,128]{1,2,0:T(8,128)(2,1)} all-to-all(bf16[32,128,128]{1,2,0:T(8,128)(2,1)S(1)} %copy.48), channel_id=1, replica_groups=mesh['grp'=4,'tp'=32,'rep'=2] {'tp'}, dimensions={0} | all-to-all | bytes 2097152 | tf_op jit(solution)/shard_map/all_to_all | solution.py:43
  59.0 6.8 %stack.2 = bf16[8,2048,512]{2,1,0:T(8,128)(2,1)} broadcast(bf16[2048,512]{1,0:T(8,128)(2,1)} %param.17), dimensions={1,2} | broadcast | bytes 18874368 | tf_op jit(solution)/shard_map/stack | solution.py:93
  65.8 11.7 %all-to-all-start = ((bf16[8,2048,512]{2,1,0:T(8,128)(2,1)}), bf16[8,2048,512]{2,1,0:T(8,128)(2,1)}, u32[]{:S(2)}, u32[]{:S(2)}) async-start(bf16[8,2048,512]{2,1,0:T(8,128)(2,1)} %stack.2), calls=%async_computation | async-start | bytes 33554432 | tf_op jit(solution)/shard_map/all_to_all | solution.py:92
  79.3 1.9 copy.51
  81.2 1.5 bitcast_convert_fusion
  82.7 1.9 copy.50
  84.5 99.8 %all-gather.2.cloned.1.call-done = bf16[2,1024,512]{1,2,0:T(8,128)(2,1)} async-done(((bf16[2,128,512]{1,2,0:T(8,128)(2,1)}), bf16[2,1024,512]{1,2,0:T(8,128)(2,1)}) %all-gather.2.cloned.1.call-update) | async-done | bytes 2097168 | tf_op jit(solution)/shard_map/all_gather | solution.py:17
  184.3 2.7 fusion.36
  187.7 1.6 copy.45
  189.4 4.2 while.39
  189.5 1.6 fusion.65
  191.1 2.3 exponential_reduce_fusion.2
  194.6 5.7 %while.40 = (s32[]{:T(128)}, f32[4,4,128,128]{3,2,1,0:T(8,128)}, s32[]{:T(128)}, bf16[4,4,128,128]{3,2,1,0:T(8,128)(2,1)S(1)}, bf16[4,1024,128]{2,1,0:T(8,128)(2...) while((s32[]{:T(128)}, f32[4,4,128,128]{3,2,1,0:T(8,128)}, ...), condition=%wide.region_5.6_spmd.clone, body=%wide.region_4.5_spmd.clone.sunk | while | flops 1084621952 | bytes 5006465 | solution.py:84
  194.8 5.6 fusion.69
  200.4 2.9 copy.46
  204.6 256.5 %all-to-all-done = bf16[8,2048,512]{2,1,0:T(8,128)(2,1)} async-done(((bf16[8,2048,512]{2,1,0:T(8,128)(2,1)}), bf16[8,2048,512]{2,1,0:T(8,128)(2,1)}, u32[]{:S(2)}, u32[]{:S(2)}) %all-to-all-start) | async-done | bytes 16777248 | tf_op jit(solution)/shard_map/all_to_all | solution.py:92
  461.0 24.1 %convert_reduce_fusion = bf16[128,2048]{1,0:T(8,128)(2,1)} fusion(bf16[8,2048,512]{2,1,0:T(8,128)(2,1)} %all-to-all-done, f32[128,8,512]{2,0,1:T(8,128)} %copy.50, f32[128,8,512]{2,0,1:T(8,128)} %copy.51, bf16[128,2048,1]{0,1,2:T(8,128)(2,1)S(1)} %bitcast.143), kind=kOutput, calls=%fused_computation.40 | convolution fusion | flops 4300472320 | bytes 22020096 | tf_op jit(solution)/shard_map/tsc,dsc->std/dot_general | solution.py:106
  486.4 1.5 multiply_reduce_fusion
  491.7 11.0 %while.41 = (s32[]{:T(128)}, f32[4,4,128,128]{3,2,1,0:T(8,128)S(1)}, bf16[4,1024,128]{2,1,0:T(8,128)(2,1)}, bf16[4,1024,128]{2,1,0:T(8,128)(2,1)}, s32[]{:T(128)...) while((s32[]{:T(128)}, ...), condition=%wide.region_9.10_spmd.clone, body=%wide.region_8.9_spmd.clone.sunk | while | flops 2703623168 | bytes 51676348 | solution.py:137
  491.8 2.8 exponential_divide_fusion.2
  494.6 1.5 multiply_convert_fusion.2
  496.1 1.3 convolution_add_fusion.2
  497.4 2.6 convolution_bitcast_fusion.2
  500.0 2.6 fusion.80
  502.7 2.0 copy.59
  505.9 2.0 copy.60
  509.2 3.1 pad_maximum_fusion
  514.0 35.1 %reduce-scatter.2.cloned.1.call-done = bf16[2,128,512]{2,1,0:T(8,128)(2,1)} async-done(((bf16[2,1024,512]{2,1,0:T(8,128)(2,1)}), bf16[2,128,512]{2,1,0:T(8,128)(2,1)}) %reduce-scatter.2.cloned.1.call-update) | async-done | bytes 262160 | tf_op jit(solution)/shard_map/reduce_scatter | solution.py:24
  549.1 1.7 fusion.37
  (51 shorter events, 15.8 us)
Async XLA Ops:
  8.5 24.3 %all-to-all-start.2 = ((bf16[32,128,1]{1,2,0:T(2,128)(2,1)}), bf16[32,128,1]{1,2,0:T(2,128)(2,1)S(1)}, u32[]{:S(2)}, u32[]{:S(2)}) async-start(bf16[32,128,1]{1,2,0:T(2,128)(2,1)} %copy.49), calls=%async_computation.2 | async-start | bytes 32768 | tf_op jit(solution)/shard_map/all_to_all | solution.py:44
  65.8 11.7 %copy-start.4 = (bf16[1,128,512]{2,1,0:T(8,128)(2,1)S(1)}, bf16[1,128,512]{2,1,0:T(8,128)(2,1)}, u32[]{:S(2)}) copy-start(bf16[1,128,512]{2,1,0:T(8,128)(2,1)} %param.13) | copy-start | bytes 393220
  65.8 11.9 %copy-start.5 = (bf16[1,128,512]{2,1,0:T(8,128)(2,1)S(1)}, bf16[1,128,512]{2,1,0:T(8,128)(2,1)}, u32[]{:S(2)}) copy-start(bf16[1,128,512]{2,1,0:T(8,128)(2,1)} %param.14) | copy-start | bytes 393220
  65.8 12.8 %copy-start.3 = (bf16[1,128,2048]{2,1,0:T(8,128)(2,1)S(1)}, bf16[1,128,2048]{2,1,0:T(8,128)(2,1)}, u32[]{:S(2)}) copy-start(bf16[1,128,2048]{2,1,0:T(8,128)(2,1)} %param.12) | copy-start | bytes 1572868
  65.8 395.2 %all-to-all-start = ((bf16[8,2048,512]{2,1,0:T(8,128)(2,1)}), bf16[8,2048,512]{2,1,0:T(8,128)(2,1)}, u32[]{:S(2)}, u32[]{:S(2)}) async-start(bf16[8,2048,512]{2,1,0:T(8,128)(2,1)} %stack.2), calls=%async_computation | async-start | bytes 33554432 | tf_op jit(solution)/shard_map/all_to_all | solution.py:92
  77.5 106.9 %all-gather.2.cloned.1.call-start = ((), (), s32[]{:S(2)}) async-start(), calls=%async_computation.4 | async-start | bytes 2359296 | tf_op jit(solution)/shard_map/all_gather | solution.py:17
  78.5 470.5 %reduce-scatter.2.cloned.1.call-start = ((), (), s32[]{:S(2)}) async-start(), calls=%async_computation.5 | async-start | bytes 2359296 | tf_op jit(solution)/shard_map/reduce_scatter | solution.py:24
  200.3 284.7 %copy-start = (bf16[4,1024,128]{2,1,0:T(8,128)(2,1)}, bf16[4,1024,128]{2,1,0:T(8,128)(2,1)S(1)}, u32[]{:S(2)}) copy-start(bf16[4,1024,128]{2,1,0:T(8,128)(2,1)S(1)} %get-tuple-element.647) | copy-start | bytes 3145732
  486.4 1.6 copy-start.2
  491.8 2.8 copy-start.1
Sparse Core Ops, SparseCore 0:
  80.6 103.7 all-gather.1
  512.4 36.6 reduce-scatter.1
